TPU v7x, 256 devices: a whole 4x4x8 slice. The times are simulated.
256 devices in a mesh: seq: 32 (over y, x, core), grp: 8 (over z).
Axes of the slice: x: 4, y: 4, z: 8, core: 2. Of those that a mesh axis runs over, the one named last changes fastest.
Arguments:
- queries: bfloat16 [32768, 8, 128], P(('grp', 'seq')), may hold values from -6 to 6
- key_rows: bfloat16 [32768, 8, 128], P(('grp', 'seq')), may hold values from -6 to 6
- value_rows: bfloat16 [32768, 8, 256], P(('grp', 'seq')), may hold values from -6 to 6
- log_gate: float32 [8, 32768], P(None, ('grp', 'seq')), may hold values from -1.5 to 0
- beta_rate: float32 [8, 32768], P(None, ('grp', 'seq')), may hold values from 0 to 0.9
Outputs:
- outputs: bfloat16 [32768, 8, 256], P(('grp', 'seq'))
All inputs are finite; a program needn't handle non-finite values.
Results may differ from a plain program's by a relative error of at most 0.0012.
Values sent between devices are 32-bit elements; how exact they have to be, the bound alone decides.
A program may use at most 128 MiB of HBM per device.

v0:
```python
import functools

import jax
import jax.numpy as jnp
from jax import lax
from jax.experimental import pallas as pl
from jax.experimental.pallas import tpu as pltpu
from jax.sharding import Mesh
from jax.sharding import PartitionSpec as P

GRP_SEQ = ("grp", "seq_0", "seq_1", "seq_2")
MESH = pl.DeviceIdType.MESH
F32 = jnp.float32
BF16 = jnp.bfloat16

T = 128
K = 128
V = 256
H = 8
HH = 4
Q = 64
ROWS = V + K


def dot(a, b):
    return lax.dot_general(a, b, (((1,), (0,)), ((), ())), preferred_element_type=F32)


def dot_nt(a, b):
    return lax.dot_general(a, b, (((1,), (1,)), ((), ())), preferred_element_type=F32)


def split(x):
    high = x.astype(BF16)
    low = (x - high.astype(F32)).astype(BF16)
    return high, low


def side(x):
    return jnp.concatenate(split(x), axis=1)


def fold(wide):
    half = wide.shape[1] // 2
    return wide[:, :half] + wide[:, half:]


def weights(w):
    pair = side(w)
    return jnp.concatenate([pair, pair], axis=0)


def mm(x, w):
    return fold(dot(side(x), weights(w)))


def mm_nt(x, y):
    wide = side(x)
    high, low = split(y)
    return dot_nt(wide, jnp.concatenate([high, high], axis=1)) + dot_nt(
        wide, jnp.concatenate([low, low], axis=1)
    )


def local_kernel(
    q_ref, k_ref, v_ref, lg_ref, be_ref, m_ref, eq_ref, lo_ref, qf, kf, vf0, vf1
):
    kf[...] = k_ref[...].astype(F32).reshape(T * H, K)
    vf0[...] = v_ref[:, :, :K].astype(F32).reshape(T * H, K)
    vf1[...] = v_ref[:, :, K:].astype(F32).reshape(T * H, K)
    qf[...] = q_ref[...].astype(F32).reshape(T * H, K)
    rows_idx = lax.broadcasted_iota(jnp.int32, (T, T), 0)
    cols_idx = lax.broadcasted_iota(jnp.int32, (T, T), 1)
    differ = rows_idx ^ cols_idx
    upper = rows_idx < cols_idx
    upper_incl = rows_idx <= cols_idx
    lower_incl = rows_idx >= cols_idx
    eye = (rows_idx == cols_idx).astype(F32)
    beta = be_ref[...]
    cum = jnp.dot(
        lg_ref[...],
        upper_incl.astype(F32),
        precision=lax.Precision.HIGHEST,
        preferred_element_type=F32,
    )

    heads = range(H)
    key = [kf[pl.ds(h, T, stride=H), :] for h in heads]
    key_b = [key[h].astype(BF16) for h in heads]
    key_t = [key[h].T for h in heads]
    squares = jnp.concatenate(
        [jnp.sum(key_t[h] * key_t[h], axis=0, keepdims=True) for h in heads], axis=0
    )
    key_tb = [key_t[h].astype(BF16) for h in heads]
    rk = 1.0 / jnp.sqrt(squares + 1e-06)
    columns = jnp.concatenate([rk, beta, cum, jnp.zeros((T - 3 * H, T), F32)], axis=0).T
    rk_col = [columns[:, h : h + 1] for h in heads]
    be_col = [columns[:, H + h : H + h + 1] for h in heads]
    cum_col = [columns[:, 2 * H + h : 2 * H + h + 1] for h in heads]
    rk_row = [rk[h : h + 1, :] for h in heads]
    be_row = [beta[h : h + 1, :] for h in heads]
    cum_row = [cum[h : h + 1, :] for h in heads]

    strict = [
        jnp.where(
            upper, dot_nt(key_b[h], key_b[h]) * rk_col[h] * (be_row[h] * rk_row[h]), 0.0
        )
        for h in heads
    ]
    inverse = [eye - jnp.where(differ == 1, strict[h], 0.0) for h in heads]
    span = 2
    while span < T:
        level = (differ >= span) & (differ < 2 * span)
        left = [mm(inverse[h], jnp.where(level, strict[h], 0.0)) for h in heads]
        inverse = [inverse[h] - mm(left[h], inverse[h]) for h in heads]
        span = span * 2

    for h in heads:
        gap = jnp.where(upper_incl, cum_row[h] - cum_col[h], 0.0)
        decay_t = jnp.where(upper_incl, jnp.exp(gap), 0.0)
        value_t = jnp.concatenate(
            [vf0[pl.ds(h, T, stride=H), :].T, vf1[pl.ds(h, T, stride=H), :].T], axis=0
        ).astype(BF16)
        w_t = fold(dot(key_tb[h], side(inverse[h] * (be_col[h] * rk_col[h]))))
        u_t = fold(dot(value_t, side(inverse[h] * decay_t * be_col[h])))
        last = cum[h : h + 1, T - 1 : T]
        into = jnp.concatenate(
            [
                u_t * (rk_row[h] * jnp.exp(last - cum_row[h])),
                w_t * (rk_row[h] * -jnp.exp(last)),
            ],
            axis=0,
        )
        moved = dot(side(into), jnp.concatenate([key_b[h], key_b[h]], axis=0))
        m_ref[h, :V, :] = moved[:V]
        m_ref[h, V:, :] = moved[V:] + eye * jnp.exp(last)

        query = qf[pl.ds(h, T, stride=H), :]
        rq = 1.0 / jnp.sqrt(jnp.sum(query * query, axis=1, keepdims=True) + 1e-06)
        seen = jnp.where(
            lower_incl, dot_nt(query.astype(BF16), key_b[h]) * rq * rk_row[h], 0.0
        )
        gap = jnp.where(lower_incl, cum_col[h] - cum_row[h], 0.0)
        eq_ref[h] = jnp.exp(cum_col[h]) * (query * rq - mm_nt(seen, w_t))
        lo_ref[h] = mm_nt(seen * jnp.exp(gap), u_t)


def joined(earlier, later):
    top = later.shape[0] - K
    moved = mm(earlier, later[top:])
    return jnp.concatenate([moved[:top] + later[:top], moved[top:]], axis=0)


def entered(state, before):
    top = before.shape[0] - K
    return mm(state, before[top:]) + before[:top]


def scan_kernel(
    m_ref,
    s_ref,
    pair,
    chip,
    row,
    row_10,
    row_210,
    row_all,
    y_send,
    y_buf,
    z_in,
    z_out,
    r_send,
    r_buf,
    x_send,
    x_buf,
    c_send,
    full,
    core_sem,
    xa_sem,
    ya_sem,
    z_sem,
    yb_sem,
    xb_sem,
    back_sem,
):
    y = lax.axis_index("seq_0")
    x = lax.axis_index("seq_1")
    c = lax.axis_index("seq_2")
    z = lax.axis_index("grp")
    planes = lax.axis_size("grp")

    def turn(at, o):
        return lax.rem(at + o + 4, 4)

    barrier = pltpu.get_barrier_semaphore()
    peers = [{"seq_2": 1 - c}]
    peers += [{"seq_1": turn(x, o)} for o in (1, 2, 3)]
    peers += [{"seq_0": turn(y, o)} for o in (1, 2, 3)]
    peers += [{"grp": lax.rem(z + 1, planes)}, {"grp": lax.rem(z + planes - 1, planes)}]
    for peer in peers:
        pl.semaphore_signal(barrier, inc=1, device_id=peer, device_id_type=MESH)
    pl.semaphore_wait(barrier, len(peers))

    def copy(src, dst, sem, o, peer):
        return pltpu.make_async_remote_copy(
            src_ref=src,
            dst_ref=dst,
            send_sem=sem.at[0, o],
            recv_sem=sem.at[1, o],
            device_id=peer,
            device_id_type=MESH,
        )

    started = []

    order = (2, 1, 3, 0)
    swaps = {}
    for o in order:
        j = turn(x, o)
        swaps[o] = copy(
            m_ref.at[HH * (1 - c) + j], pair.at[c, j], core_sem, o, {"seq_2": 1 - c}
        )
        swaps[o].start()
        started.append(swaps[o])
    for o in order:
        j = turn(x, o)
        pair[c, j] = m_ref[HH * c + j]
    sends = {}
    for o in order:
        j = turn(x, o)
        swaps[o].wait_recv()
        both = joined(pair[0, j], pair[1, j])
        if o == 0:
            row[x] = both
        else:
            chip[o] = both
            sends[o] = copy(chip.at[o], row.at[x], xa_sem, o, {"seq_1": j})
            sends[o].start()
            started.append(sends[o])
    for o in (1, 3, 2):
        sends[o].wait_recv()

    row_10[...] = joined(row[0], row[1])
    row_32 = joined(row[2], row[3])
    row_all[...] = joined(row_10[...], row_32)

    sends = {}
    for o in (2, 1, 3):
        to = turn(y, o)
        y_send[o, :Q, :] = row_all[pl.ds(pl.multiple_of(to * Q, Q), Q), :]
        y_send[o, Q:, :] = row_all[V:, :]
        sends[o] = copy(y_send.at[o], y_buf.at[y], ya_sem, o, {"seq_0": to})
        sends[o].start()
        started.append(sends[o])
    y_buf[y, :Q, :] = row_all[pl.ds(pl.multiple_of(y * Q, Q), Q), :]
    y_buf[y, Q:, :] = row_all[V:, :]
    row_210[...] = joined(row_10[...], row[2])
    for o in (1, 3, 2):
        sends[o].wait_recv()
    plane_10 = joined(y_buf[0], y_buf[1])
    plane_32 = joined(y_buf[2], y_buf[3])
    plane = joined(plane_10, plane_32)

    hop = copy(z_out, z_in, z_sem, 0, {"grp": lax.rem(z + 1, planes)})

    @pl.when(z == 0)
    def _():
        z_in[...] = jnp.zeros_like(z_in)

    @pl.when(z > 0)
    def _():
        hop.wait_recv()

    state = z_in[...]

    @pl.when(z < planes - 1)
    def _():
        z_out[...] = entered(state, plane)
        hop.start()

    plane_210 = joined(plane_10, y_buf[2])
    r_send[0] = state
    r_send[1] = entered(state, y_buf[0])
    r_send[2] = entered(state, plane_10)
    r_send[3] = entered(state, plane_210)
    mine = pl.ds(pl.multiple_of(y * Q, Q), Q)
    sends = {}
    for o in (2, 1, 3):
        to = turn(y, o)
        sends[o] = copy(r_send.at[to], r_buf.at[mine], yb_sem, o, {"seq_0": to})
        sends[o].start()
        started.append(sends[o])
    r_buf[mine, :] = r_send[y]
    for o in (1, 3, 2):
        sends[o].wait_recv()

    state = r_buf[...]
    x_send[0] = state
    x_send[1] = entered(state, row[0])
    x_send[2] = entered(state, row_10[...])
    x_send[3] = entered(state, row_210[...])
    sends = {}
    for o in (2, 1, 3):
        to = turn(x, o)
        sends[o] = copy(x_send.at[to], x_buf.at[x], xb_sem, o, {"seq_1": to})
        sends[o].start()
        started.append(sends[o])
    x_buf[x] = x_send[x]

    swaps = []
    for o in (0, 1, 3, 2):
        j = turn(x, -o)
        if o > 0:
            sends[o].wait_recv()
        first = x_buf[j]
        second = entered(first, pair[0, j])
        head = HH * c + j
        full[head] = jnp.where(c == 0, first, second)
        c_send[o] = jnp.where(c == 0, second, first)
        swap = copy(c_send.at[o], full.at[head], back_sem, o, {"seq_2": 1 - c})
        swap.start()
        started.append(swap)
        swaps.append(swap)
    for swap in swaps:
        swap.wait_recv()
    s_ref[...] = full[...]

    for sent in started:
        sent.wait_send()

    @pl.when(z < planes - 1)
    def _():
        hop.wait_send()


def final_kernel(eq_ref, lo_ref, s_ref, o_ref, of0, of1):
    for h in range(H):
        both = lo_ref[h] + mm_nt(eq_ref[h], s_ref[h])
        of0[pl.ds(h, T, stride=H), :] = both[:, :K]
        of1[pl.ds(h, T, stride=H), :] = both[:, K:]
    o_ref[:, :, :K] = of0[...].reshape(T, H, K).astype(BF16)
    o_ref[:, :, K:] = of1[...].reshape(T, H, K).astype(BF16)


VM = pl.BlockSpec(memory_space=pltpu.VMEM)


def body(queries, key_rows, value_rows, log_gate, beta_rate):
    maps, eff_query, local_out = pl.pallas_call(
        local_kernel,
        out_shape=(
            jax.ShapeDtypeStruct((H, ROWS, K), F32),
            jax.ShapeDtypeStruct((H, T, K), F32),
            jax.ShapeDtypeStruct((H, T, V), F32),
        ),
        in_specs=[VM] * 5,
        out_specs=(VM, VM, VM),
        scratch_shapes=[pltpu.VMEM((T * H, K), F32)] * 4,
        compiler_params=pltpu.CompilerParams(vmem_limit_bytes=48 * 1024 * 1024),
        name="local",
    )(queries, key_rows, value_rows, log_gate, beta_rate)
    dma = pltpu.SemaphoreType.DMA
    states = pl.pallas_call(
        scan_kernel,
        out_shape=jax.ShapeDtypeStruct((H, V, K), F32),
        in_specs=[VM],
        out_specs=VM,
        scratch_shapes=[
            pltpu.VMEM((2, HH, ROWS, K), F32),
            pltpu.VMEM((4, ROWS, K), F32),
            pltpu.VMEM((4, ROWS, K), F32),
            pltpu.VMEM((ROWS, K), F32),
            pltpu.VMEM((ROWS, K), F32),
            pltpu.VMEM((ROWS, K), F32),
            pltpu.VMEM((4, Q + K, K), F32),
            pltpu.VMEM((4, Q + K, K), F32),
            pltpu.VMEM((Q, K), F32),
            pltpu.VMEM((Q, K), F32),
            pltpu.VMEM((4, Q, K), F32),
            pltpu.VMEM((V, K), F32),
            pltpu.VMEM((4, V, K), F32),
            pltpu.VMEM((4, V, K), F32),
            pltpu.VMEM((4, V, K), F32),
            pltpu.VMEM((H, V, K), F32),
            dma((2, 4)),
            dma((2, 4)),
            dma((2, 4)),
            dma((2, 1)),
            dma((2, 4)),
            dma((2, 4)),
            dma((2, 4)),
        ],
        compiler_params=pltpu.CompilerParams(
            collective_id=0, has_side_effects=True, vmem_limit_bytes=48 * 1024 * 1024
        ),
        name="scan",
    )(maps)
    return pl.pallas_call(
        final_kernel,
        out_shape=jax.ShapeDtypeStruct((T, H, V), BF16),
        in_specs=[VM] * 3,
        out_specs=VM,
        scratch_shapes=[pltpu.VMEM((T * H, K), F32)] * 2,
        compiler_params=pltpu.CompilerParams(vmem_limit_bytes=48 * 1024 * 1024),
        name="final",
    )(eff_query, local_out, states)


def solution(mesh):
    finer = Mesh(
        mesh.devices.reshape(4, 4, 2, mesh.shape["grp"]), ("seq_0", "seq_1", "seq_2", "grp")
    )
    placed = (
        P(GRP_SEQ, None, None),
        P(GRP_SEQ, None, None),
        P(GRP_SEQ, None, None),
        P(None, GRP_SEQ),
        P(None, GRP_SEQ),
    )
    return jax.shard_map(
        body, mesh=finer, in_specs=placed, out_specs=P(GRP_SEQ, None, None), check_vma=False
    )
```

profile of v0, /device:TPU:227, one launch (start us, length us, event | category | flops | bytes accessed | tf_op | source)
XLA Modules:
  0.0 70.1 jit_solution(9830727361960452535)
XLA Ops:
  0.0 0.0 copy-start
  0.0 1.0 %copy-done = bf16[128,8,256]{2,1,0:T(8,128)(2,1)S(1)} copy-done((bf16[128,8,256]{2,1,0:T(8,128)(2,1)S(1)}, bf16[128,8,256]{2,1,0:T(8,128)(2,1)}, u32[]{:S(2)}) %copy-start) | copy-done | bytes 524312
  1.0 0.0 copy-start.1
  1.0 0.9 %copy-done.1 = bf16[128,8,128]{2,1,0:T(8,128)(2,1)S(1)} copy-done((bf16[128,8,128]{2,1,0:T(8,128)(2,1)S(1)}, bf16[128,8,128]{2,1,0:T(8,128)(2,1)}, u32[]{:S(2)}) %copy-start.1) | copy-done | bytes 262168
  2.0 0.0 copy-start.2
  2.0 0.9 %copy-done.2 = bf16[128,8,128]{2,1,0:T(8,128)(2,1)S(1)} copy-done((bf16[128,8,128]{2,1,0:T(8,128)(2,1)S(1)}, bf16[128,8,128]{2,1,0:T(8,128)(2,1)}, u32[]{:S(2)}) %copy-start.2) | copy-done | bytes 262168
  2.9 0.0 copy-start.3
  2.9 0.7 copy-done.3
  3.6 0.0 copy-start.4
  3.6 0.7 copy-done.4
  4.3 5.7 %local.1 = (f32[8,384,128]{2,1,0:T(8,128)S(1)}, f32[8,128,128]{2,1,0:T(8,128)S(1)}, f32[8,128,256]{2,1,0:T(8,128)S(1)}) custom-call(bf16[128,8,128]{2,1,0:T(8,128)(2,1)S(1)} %copy-done.1, bf16[128,8,128]{2,1,0:T(8,128)(2,1)S(1)} %copy-done.2, bf16[128,8,256]{2,1,0:T(8,128)(2,1)S(1)} %copy-done, f32[8,128]{1,0:T(8,128)S(1)} %copy-done.3, f32[8,128]{1,0:T(8,128)S(1)} %copy-done.4), custom_call_target="tpu_custom_call" | custom-call | tf_op jit(solution)/shard_map/local/pallas_call | solution.py:349
  10.0 58.4 %scan.1.s_ref = f32[8,256,128]{2,1,0:T(8,128)S(1)} custom-call(f32[8,384,128]{2,1,0:T(8,128)S(1)} %get-tuple-element.10.m_ref), custom_call_target="tpu_custom_call" | custom-call | tf_op jit(solution)/shard_map/scan/pallas_call | solution.py:363
  68.4 1.7 %final.1 = bf16[128,8,256]{2,1,0:T(8,128)(2,1)} custom-call(f32[8,128,128]{2,1,0:T(8,128)S(1)} %get-tuple-element.8.eq_ref, f32[8,128,256]{2,1,0:T(8,128)S(1)} %get-tuple-element.9.lo_ref, f32[8,256,128]{2,1,0:T(8,128)S(1)} %scan.1.s_ref), custom_call_target="tpu_custom_call" | custom-call | tf_op jit(solution)/shard_map/final/pallas_call | solution.py:398
Async XLA Ops:
  0.0 1.0 %copy-start = (bf16[128,8,256]{2,1,0:T(8,128)(2,1)S(1)}, bf16[128,8,256]{2,1,0:T(8,128)(2,1)}, u32[]{:S(2)}) copy-start(bf16[128,8,256]{2,1,0:T(8,128)(2,1)} %v_ref.1) | copy-start | bytes 1572868
  1.0 0.9 %copy-start.1 = (bf16[128,8,128]{2,1,0:T(8,128)(2,1)S(1)}, bf16[128,8,128]{2,1,0:T(8,128)(2,1)}, u32[]{:S(2)}) copy-start(bf16[128,8,128]{2,1,0:T(8,128)(2,1)} %q_ref.1) | copy-start | bytes 786436
  2.0 0.9 %copy-start.2 = (bf16[128,8,128]{2,1,0:T(8,128)(2,1)S(1)}, bf16[128,8,128]{2,1,0:T(8,128)(2,1)}, u32[]{:S(2)}) copy-start(bf16[128,8,128]{2,1,0:T(8,128)(2,1)} %k_ref.1) | copy-start | bytes 786436
  2.9 0.7 copy-start.3
  3.6 0.7 copy-start.4
where the time goes:
time: 70.3 us; the launch traced here: 70.1 us
  Pallas kernels  65.8 us (94%)
  local copies, waits for them, and re-layouts  4.31 us (6%)
    pallas_call x1, Pallas kernels, body(): pl.pallas_call(scan_kernel, out_shape=jax.ShapeDtypeStruct((H, V, K), F32...  58.4 us
    pallas_call x1, Pallas kernels, body(): pl.pallas_call(local_kernel, out_shape=(jax.ShapeDtypeStruct((H, ROWS, K)...  5.68 us
    unnamed x10, local copies, waits for them, and re-layouts  4.31 us
    pallas_call x1, Pallas kernels, body(): pl.pallas_call(final_kernel, out_shape=jax.ShapeDtypeStruct((T, H, V), BF...  1.73 us

commit v1 on v0

v1 whole, which is shorter than its diff:
```python
import functools

import jax
import jax.numpy as jnp
from jax import lax
from jax.experimental import pallas as pl
from jax.experimental.pallas import tpu as pltpu
from jax.sharding import Mesh
from jax.sharding import PartitionSpec as P

GRP_SEQ = ("grp", "seq_0", "seq_1", "seq_2")
MESH = pl.DeviceIdType.MESH
F32 = jnp.float32
BF16 = jnp.bfloat16

T = 128
K = 128
V = 256
H = 8
HH = 4
Q = 64
ROWS = V + K


def dot(a, b):
    return lax.dot_general(a, b, (((1,), (0,)), ((), ())), preferred_element_type=F32)


def dot_nt(a, b):
    return lax.dot_general(a, b, (((1,), (1,)), ((), ())), preferred_element_type=F32)


def split(x):
    high = x.astype(BF16)
    low = (x - high.astype(F32)).astype(BF16)
    return high, low


def side(x):
    return jnp.concatenate(split(x), axis=1)


def fold(wide):
    half = wide.shape[1] // 2
    return wide[:, :half] + wide[:, half:]


def weights(w):
    pair = side(w)
    return jnp.concatenate([pair, pair], axis=0)


def mm(x, w):
    return fold(dot(side(x), weights(w)))


def mm_nt(x, y):
    wide = side(x)
    high, low = split(y)
    return dot_nt(wide, jnp.concatenate([high, high], axis=1)) + dot_nt(
        wide, jnp.concatenate([low, low], axis=1)
    )


def joined(earlier, later):
    top = later.shape[0] - K
    moved = mm(earlier, later[top:])
    return jnp.concatenate([moved[:top] + later[:top], moved[top:]], axis=0)


def entered(state, before):
    top = before.shape[0] - K
    return mm(state, before[top:]) + before[:top]


def turn(at, o):
    return lax.rem(at + o + 4, 4)


def scan_kernel(
    q_ref,
    k_ref,
    v_ref,
    lg_ref,
    be_ref,
    o_ref,
    q_in,
    k_in,
    v_in,
    lg_in,
    be_in,
    qf,
    kf,
    vf0,
    vf1,
    w_all,
    u_all,
    eff,
    own,
    maps,
    pair,
    chip,
    row,
    row_10,
    row_210,
    row_all,
    y_send,
    y_buf,
    p_send,
    p_buf,
    z_in,
    z_out,
    enter,
    r_send,
    r_buf,
    x_send,
    x_buf,
    c_send,
    full,
    in_sem,
    core_sem,
    xa_sem,
    ya_sem,
    p_sem,
    z_sem,
    yb_sem,
    xb_sem,
    back_sem,
):
    y = lax.axis_index("seq_0")
    x = lax.axis_index("seq_1")
    c = lax.axis_index("seq_2")
    z = lax.axis_index("grp")
    planes = lax.axis_size("grp")
    heads = range(H)

    loads = []
    for i, (src, dst) in enumerate(
        ((k_ref, k_in), (lg_ref, lg_in), (be_ref, be_in), (v_ref, v_in), (q_ref, q_in))
    ):
        loads.append(pltpu.make_async_copy(src, dst, in_sem.at[i]))
        loads[i].start()

    barrier = pltpu.get_barrier_semaphore()
    peers = [{"seq_2": 1 - c}]
    peers += [{"seq_1": turn(x, o)} for o in (1, 2, 3)]
    peers += [{"seq_0": turn(y, o)} for o in (1, 2, 3)]
    peers += [{"grp": lax.rem(z + planes + o, planes)} for o in (1, -1, 2, -2)]
    for peer in peers:
        pl.semaphore_signal(barrier, inc=1, device_id=peer, device_id_type=MESH)

    def copy(src, dst, sem, o, peer):
        return pltpu.make_async_remote_copy(
            src_ref=src,
            dst_ref=dst,
            send_sem=sem.at[0, o],
            recv_sem=sem.at[1, o],
            device_id=peer,
            device_id_type=MESH,
        )

    started = []

    rows_idx = lax.broadcasted_iota(jnp.int32, (T, T), 0)
    cols_idx = lax.broadcasted_iota(jnp.int32, (T, T), 1)
    differ = rows_idx ^ cols_idx
    upper = rows_idx < cols_idx
    upper_incl = rows_idx <= cols_idx
    lower_incl = rows_idx >= cols_idx
    eye = (rows_idx == cols_idx).astype(F32)
    loads[0].wait()
    kf[...] = k_in[...].astype(F32).reshape(T * H, K)
    key = [kf[pl.ds(h, T, stride=H), :] for h in heads]
    key_b = [key[h].astype(BF16) for h in heads]
    key_t = [key[h].T for h in heads]
    squares = jnp.concatenate(
        [jnp.sum(key_t[h] * key_t[h], axis=0, keepdims=True) for h in heads], axis=0
    )
    key_tb = [key_t[h].astype(BF16) for h in heads]
    loads[1].wait()
    loads[2].wait()
    beta = be_in[...]
    cum = jnp.dot(
        lg_in[...],
        upper_incl.astype(F32),
        precision=lax.Precision.HIGHEST,
        preferred_element_type=F32,
    )
    rk = 1.0 / jnp.sqrt(squares + 1e-06)
    columns = jnp.concatenate([rk, beta, cum, jnp.zeros((T - 3 * H, T), F32)], axis=0).T
    rk_col = [columns[:, h : h + 1] for h in heads]
    be_col = [columns[:, H + h : H + h + 1] for h in heads]
    cum_col = [columns[:, 2 * H + h : 2 * H + h + 1] for h in heads]
    rk_row = [rk[h : h + 1, :] for h in heads]
    be_row = [beta[h : h + 1, :] for h in heads]
    cum_row = [cum[h : h + 1, :] for h in heads]
    strict = [
        jnp.where(
            upper, dot_nt(key_b[h], key_b[h]) * rk_col[h] * (be_row[h] * rk_row[h]), 0.0
        )
        for h in heads
    ]
    inverse = [eye - jnp.where(differ == 1, strict[h], 0.0) for h in heads]
    span = 2
    while span < T:
        level = (differ >= span) & (differ < 2 * span)
        left = [mm(inverse[h], jnp.where(level, strict[h], 0.0)) for h in heads]
        inverse = [inverse[h] - mm(left[h], inverse[h]) for h in heads]
        span = span * 2
    loads[3].wait()
    vf0[...] = v_in[:, :, :K].astype(F32).reshape(T * H, K)
    vf1[...] = v_in[:, :, K:].astype(F32).reshape(T * H, K)
    for h in heads:
        gap = jnp.where(upper_incl, cum_row[h] - cum_col[h], 0.0)
        decay_t = jnp.where(upper_incl, jnp.exp(gap), 0.0)
        value_t = jnp.concatenate(
            [vf0[pl.ds(h, T, stride=H), :].T, vf1[pl.ds(h, T, stride=H), :].T], axis=0
        ).astype(BF16)
        w_t = fold(dot(key_tb[h], side(inverse[h] * (be_col[h] * rk_col[h]))))
        u_t = fold(dot(value_t, side(inverse[h] * decay_t * be_col[h])))
        last = cum[h : h + 1, T - 1 : T]
        into = jnp.concatenate(
            [
                u_t * (rk_row[h] * jnp.exp(last - cum_row[h])),
                w_t * (rk_row[h] * -jnp.exp(last)),
            ],
            axis=0,
        )
        moved = dot(side(into), jnp.concatenate([key_b[h], key_b[h]], axis=0))
        maps[h, :V, :] = moved[:V]
        maps[h, V:, :] = moved[V:] + eye * jnp.exp(last)
        w_all[h] = w_t
        u_all[h] = u_t

    pl.semaphore_wait(barrier, len(peers))

    order = (2, 1, 3, 0)
    swaps = {}
    for o in order:
        j = turn(x, o)
        swaps[o] = copy(
            maps.at[HH * (1 - c) + j], pair.at[c, j], core_sem, o, {"seq_2": 1 - c}
        )
        swaps[o].start()
        started.append(swaps[o])
    for o in order:
        j = turn(x, o)
        pair[c, j] = maps[HH * c + j]
    sends = {}
    for o in order:
        j = turn(x, o)
        swaps[o].wait_recv()
        both = joined(pair[0, j], pair[1, j])
        if o == 0:
            row[x] = both
        else:
            chip[o] = both
            sends[o] = copy(chip.at[o], row.at[x], xa_sem, o, {"seq_1": j})
            sends[o].start()
            started.append(sends[o])

    loads[4].wait()
    qf[...] = q_in[...].astype(F32).reshape(T * H, K)
    for h in heads:
        query = qf[pl.ds(h, T, stride=H), :]
        key_h = kf[pl.ds(h, T, stride=H), :].astype(BF16)
        rq = 1.0 / jnp.sqrt(jnp.sum(query * query, axis=1, keepdims=True) + 1e-06)
        seen = jnp.where(
            lower_incl, dot_nt(query.astype(BF16), key_h) * rq * rk_row[h], 0.0
        )
        gap = jnp.where(lower_incl, cum_col[h] - cum_row[h], 0.0)
        eff[h] = jnp.exp(cum_col[h]) * (query * rq - mm_nt(seen, w_all[h]))
        own[h] = mm_nt(seen * jnp.exp(gap), u_all[h])

    for o in (1, 3, 2):
        sends[o].wait_recv()

    row_10[...] = joined(row[0], row[1])
    row_32 = joined(row[2], row[3])
    row_all[...] = joined(row_10[...], row_32)

    sends = {}
    for o in (2, 1, 3):
        to = turn(y, o)
        y_send[o, :Q, :] = row_all[pl.ds(pl.multiple_of(to * Q, Q), Q), :]
        y_send[o, Q:, :] = row_all[V:, :]
        sends[o] = copy(y_send.at[o], y_buf.at[y], ya_sem, o, {"seq_0": to})
        sends[o].start()
        started.append(sends[o])
    y_buf[y, :Q, :] = row_all[pl.ds(pl.multiple_of(y * Q, Q), Q), :]
    y_buf[y, Q:, :] = row_all[V:, :]
    row_210[...] = joined(row_10[...], row[2])
    for o in (1, 3, 2):
        sends[o].wait_recv()
    plane_10 = joined(y_buf[0], y_buf[1])
    plane_32 = joined(y_buf[2], y_buf[3])
    plane = joined(plane_10, plane_32)

    odd = lax.rem(z, 2) == 1
    next_one = {"grp": lax.rem(z + 1, planes)}
    give_state = copy(p_send.at[pl.ds(0, Q)], p_buf.at[pl.ds(0, Q)], p_sem, 0, next_one)
    give_trans = copy(p_send.at[pl.ds(Q, K)], p_buf.at[pl.ds(Q, K)], p_sem, 1, next_one)
    jump = copy(z_out, z_in, z_sem, 0, {"grp": lax.rem(z + 2, planes)})
    step = copy(z_out, z_in, z_sem, 1, next_one)

    @pl.when(jnp.logical_not(odd))
    def _():
        p_send[...] = plane
        give_state.start()
        give_trans.start()

    plane_210 = joined(plane_10, y_buf[2])

    @pl.when(z == 0)
    def _():
        enter[...] = jnp.zeros_like(enter)

    @pl.when(z == 1)
    def _():
        give_state.wait_recv()
        z_out[...] = entered(p_buf[:Q, :], plane)
        jump.start()
        step.start()
        enter[...] = p_buf[:Q, :]
        give_trans.wait_recv()

    @pl.when(odd & (z > 1))
    def _():
        give_state.wait_recv()
        give_trans.wait_recv()
        two = joined(p_buf[...], plane)
        jump.wait_recv()

        @pl.when(z < planes - 1)
        def _():
            z_out[...] = entered(z_in[...], two)

            @pl.when(z < planes - 2)
            def _():
                jump.start()

            step.start()

        enter[...] = entered(z_in[...], p_buf[...])

    @pl.when(jnp.logical_not(odd) & (z > 0))
    def _():
        step.wait_recv()
        enter[...] = z_in[...]

    state = enter[...]
    r_send[0] = state
    r_send[1] = entered(state, y_buf[0])
    r_send[2] = entered(state, plane_10)
    r_send[3] = entered(state, plane_210)
    mine = pl.ds(pl.multiple_of(y * Q, Q), Q)
    sends = {}
    for o in (2, 1, 3):
        to = turn(y, o)
        sends[o] = copy(r_send.at[to], r_buf.at[mine], yb_sem, o, {"seq_0": to})
        sends[o].start()
        started.append(sends[o])
    r_buf[mine, :] = r_send[y]
    arrivals = {1: [], 2: [], 3: []}
    for o in (0, 1, 3, 2):
        if o > 0:
            sends[o].wait_recv()
        part = pl.ds(pl.multiple_of(turn(y, -o) * Q, Q), Q)
        state = r_buf[part, :]
        x_send[0, part, :] = state
        x_send[1, part, :] = mm(state, row[0, V:, :]) + row[0, part, :]
        x_send[2, part, :] = mm(state, row_10[V:, :]) + row_10[part, :]
        x_send[3, part, :] = mm(state, row_210[V:, :]) + row_210[part, :]
        for a in (2, 1, 3):
            to = turn(x, a)
            sent = copy(
                x_send.at[to, part], x_buf.at[x, part], xb_sem, 4 * a + o, {"seq_1": to}
            )
            sent.start()
            started.append(sent)
            arrivals[a].append(sent)
        x_buf[x, part, :] = x_send[x, part, :]

    def read_out(head):
        both = own[head] + mm_nt(eff[head], full[head])
        vf0[pl.ds(head, T, stride=H), :] = both[:, :K]
        vf1[pl.ds(head, T, stride=H), :] = both[:, K:]

    swaps = []
    for a in (0, 1, 3, 2):
        j = turn(x, -a)
        if a > 0:
            for sent in arrivals[a]:
                sent.wait_recv()
        first = x_buf[j]
        second = entered(first, pair[0, j])
        head = HH * c + j
        full[head] = jnp.where(c == 0, first, second)
        c_send[a] = jnp.where(c == 0, second, first)
        swap = copy(c_send.at[a], full.at[head], back_sem, a, {"seq_2": 1 - c})
        swap.start()
        started.append(swap)
        swaps.append((swap, j))
        read_out(head)
    for swap, j in swaps:
        swap.wait_recv()
        read_out(HH * (1 - c) + j)
    o_ref[:, :, :K] = vf0[...].reshape(T, H, K).astype(BF16)
    o_ref[:, :, K:] = vf1[...].reshape(T, H, K).astype(BF16)

    for sent in started:
        sent.wait_send()

    @pl.when(jnp.logical_not(odd))
    def _():
        give_state.wait_send()
        give_trans.wait_send()

    @pl.when(odd & (z < planes - 1))
    def _():
        step.wait_send()

    @pl.when(odd & (z < planes - 2))
    def _():
        jump.wait_send()


def body(*given):
    queries, key_rows, value_rows, log_gate, beta_rate = [pltpu.with_memory_space_constraint(a, pltpu.HBM) for a in given]
    dma = pltpu.SemaphoreType.DMA

    def room(*shape):
        return pltpu.VMEM(shape, F32)

    return pl.pallas_call(
        scan_kernel,
        out_shape=jax.ShapeDtypeStruct((T, H, V), BF16),
        in_specs=[pl.BlockSpec(memory_space=pltpu.HBM)] * 5,
        out_specs=pl.BlockSpec(memory_space=pltpu.VMEM),
        scratch_shapes=[
            pltpu.VMEM((T, H, K), BF16),
            pltpu.VMEM((T, H, K), BF16),
            pltpu.VMEM((T, H, V), BF16),
            room(H, T),
            room(H, T),
            room(T * H, K),
            room(T * H, K),
            room(T * H, K),
            room(T * H, K),
            room(H, K, T),
            room(H, V, T),
            room(H, T, K),
            room(H, T, V),
            room(H, ROWS, K),
            room(2, HH, ROWS, K),
            room(4, ROWS, K),
            room(4, ROWS, K),
            room(ROWS, K),
            room(ROWS, K),
            room(ROWS, K),
            room(4, Q + K, K),
            room(4, Q + K, K),
            room(Q + K, K),
            room(Q + K, K),
            room(Q, K),
            room(Q, K),
            room(Q, K),
            room(4, Q, K),
            room(V, K),
            room(4, V, K),
            room(4, V, K),
            room(4, V, K),
            room(H, V, K),
            dma((5,)),
            dma((2, 4)),
            dma((2, 4)),
            dma((2, 4)),
            dma((2, 2)),
            dma((2, 2)),
            dma((2, 4)),
            dma((2, 16)),
            dma((2, 4)),
        ],
        compiler_params=pltpu.CompilerParams(
            collective_id=0, has_side_effects=True, vmem_limit_bytes=48 * 1024 * 1024
        ),
        name="scan",
    )(queries, key_rows, value_rows, log_gate, beta_rate)


def solution(mesh):
    finer = Mesh(
        mesh.devices.reshape(4, 4, 2, mesh.shape["grp"]), ("seq_0", "seq_1", "seq_2", "grp")
    )
    placed = (
        P(GRP_SEQ, None, None),
        P(GRP_SEQ, None, None),
        P(GRP_SEQ, None, None),
        P(None, GRP_SEQ),
        P(None, GRP_SEQ),
    )
    return jax.shard_map(
        body, mesh=finer, in_specs=placed, out_specs=P(GRP_SEQ, None, None), check_vma=False
    )
```

time: 70.3 us -> 51.6 us (0.73)
  Pallas kernels: 65.8 us -> 50.5 us
  local copies, waits for them, and re-layouts: 4.31 us -> 0.8 us
    pallas_call x3 -> x1, Pallas kernels: 65.8 us -> 50.5 us  [body(): pl.pallas_call(scan_kernel, out_shape=jax.ShapeDtypeStruct((T, H, V), BF1...]
    unnamed x10 -> x1, local copies, waits for them, and re-layouts: 4.31 us -> 0.8 us
where the time goes in v1:
time: 51.6 us; the launch traced here: 51.3 us
  Pallas kernels  50.5 us (98%)
  local copies, waits for them, and re-layouts  0.8 us (2%)
    pallas_call x1, Pallas kernels, body(): pl.pallas_call(scan_kernel, out_shape=jax.ShapeDtypeStruct((T, H, V), BF1...  50.5 us

profile of v1, /device:TPU:227, one launch (start us, length us, event | category | flops | bytes accessed | tf_op | source)
XLA Modules:
  0.0 51.3 jit_solution(10403847127894091734)
XLA Ops:
  0.0 50.5 %scan.1 = bf16[128,8,256]{2,1,0:T(8,128)(2,1)S(1)} custom-call(bf16[128,8,128]{2,1,0:T(8,128)(2,1)} %q_ref.1, bf16[128,8,128]{2,1,0:T(8,128)(2,1)} %k_ref.1, bf16[128,8,256]{2,1,0:T(8,128)(2,1)} %v_ref.1, f32[8,128]{1,0:T(8,128)} %lg_ref.1, f32[8,128]{1,0:T(8,128)} %be_ref.1), custom_call_target="tpu_custom_call" | custom-call | tf_op jit(solution)/shard_map/scan/pallas_call | solution.py:435
  50.5 0.8 %copy.7 = bf16[128,8,256]{2,1,0:T(8,128)(2,1)} copy(bf16[128,8,256]{2,1,0:T(8,128)(2,1)S(1)} %scan.1) | data formatting | bytes 1048576

commit v2 on v1

--- a/solution.py
+++ b/solution.py
@@ -235,29 +235,62 @@
     pl.semaphore_wait(barrier, len(peers))
 
     order = (2, 1, 3, 0)
+    tail = pl.ds(V, K)
+    body_rows = pl.ds(0, V)
     swaps = {}
-    for o in order:
-        j = turn(x, o)
-        swaps[o] = copy(
-            maps.at[HH * (1 - c) + j], pair.at[c, j], core_sem, o, {"seq_2": 1 - c}
-        )
-        swaps[o].start()
-        started.append(swaps[o])
+    for i, rows in ((0, tail), (4, body_rows)):
+        for o in order:
+            j = turn(x, o)
+            swaps[i + o] = copy(
+                maps.at[HH * (1 - c) + j, rows],
+                pair.at[c, j, rows],
+                core_sem,
+                i + o,
+                {"seq_2": 1 - c},
+            )
+            swaps[i + o].start()
+            started.append(swaps[i + o])
     for o in order:
         j = turn(x, o)
         pair[c, j] = maps[HH * c + j]
+
+    def along_x(o, rows, slot):
+        sent = copy(
+            chip.at[o, rows],
+            row.at[x, rows],
+            xa_sem,
+            5 * (o - 1) + slot,
+            {"seq_1": turn(x, o)},
+        )
+        sent.start()
+        started.append(sent)
+        return sent
+
+    def quarter(o):
+        return pl.ds(pl.multiple_of(turn(y, o) * Q, Q), Q)
+
     sends = {}
     for o in order:
         j = turn(x, o)
         swaps[o].wait_recv()
-        both = joined(pair[0, j], pair[1, j])
+        both = mm(pair[0, j, V:, :], pair[1, j, V:, :])
         if o == 0:
-            row[x] = both
+            row[x, V:, :] = both
         else:
-            chip[o] = both
-            sends[o] = copy(chip.at[o], row.at[x], xa_sem, o, {"seq_1": j})
-            sends[o].start()
-            started.append(sends[o])
+            chip[o, V:, :] = both
+            sends[o, 4] = along_x(o, tail, 4)
+    for o in order:
+        j = turn(x, o)
+        swaps[4 + o].wait_recv()
+        both = mm(pair[0, j, :V, :], pair[1, j, V:, :]) + pair[1, j, :V, :]
+        if o == 0:
+            row[x, :V, :] = both
+        else:
+            chip[o, :V, :] = both
+            sends[o, 2] = along_x(o, quarter(2), 2)
+    for part in (1, 3, 0):
+        for o in (2, 1, 3):
+            sends[o, part] = along_x(o, quarter(part), part)
 
     loads[4].wait()
     qf[...] = q_in[...].astype(F32).reshape(T * H, K)
@@ -273,42 +306,78 @@
         own[h] = mm_nt(seen * jnp.exp(gap), u_all[h])
 
     for o in (1, 3, 2):
-        sends[o].wait_recv()
-
-    row_10[...] = joined(row[0], row[1])
-    row_32 = joined(row[2], row[3])
-    row_all[...] = joined(row_10[...], row_32)
-
-    sends = {}
+        sends[o, 4].wait_recv()
+    row_t = [row[k, V:, :] for k in range(4)]
+    row_t10 = mm(row_t[0], row_t[1])
+    row_t32 = mm(row_t[2], row_t[3])
+    row_10[V:, :] = row_t10
+    row_all[...] = mm(row_t10, row_t32)
+    gives = {}
     for o in (2, 1, 3):
-        to = turn(y, o)
-        y_send[o, :Q, :] = row_all[pl.ds(pl.multiple_of(to * Q, Q), Q), :]
-        y_send[o, Q:, :] = row_all[V:, :]
-        sends[o] = copy(y_send.at[o], y_buf.at[y], ya_sem, o, {"seq_0": to})
-        sends[o].start()
-        started.append(sends[o])
-    y_buf[y, :Q, :] = row_all[pl.ds(pl.multiple_of(y * Q, Q), Q), :]
-    y_buf[y, Q:, :] = row_all[V:, :]
-    row_210[...] = joined(row_10[...], row[2])
+        gives[o] = copy(
+            row_all, y_buf.at[y, pl.ds(Q, K)], ya_sem, o, {"seq_0": turn(y, o)}
+        )
+        gives[o].start()
+        started.append(gives[o])
+    y_buf[y, Q:, :] = row_all[...]
+    weights_1 = weights(row_t[1])
+    weights_3 = weights(row_t[3])
+    weights_32 = weights(row_t32)
+    for part in (2, 1, 3, 0):
+        rows = quarter(part)
+        for o in (1, 3, 2):
+            sends[o, part].wait_recv()
+        part_10 = fold(dot(side(row[0, rows, :]), weights_1)) + row[1, rows, :]
+        part_32 = fold(dot(side(row[2, rows, :]), weights_3)) + row[3, rows, :]
+        row_10[rows, :] = part_10
+        total = fold(dot(side(part_10), weights_32)) + part_32
+        if part == 0:
+            y_buf[y, :Q, :] = total
+        else:
+            y_send[part] = total
+            gives[4 + part] = copy(
+                y_send.at[part],
+                y_buf.at[y, pl.ds(0, Q)],
+                ya_sem,
+                4 + part,
+                {"seq_0": turn(y, part)},
+            )
+            gives[4 + part].start()
+            started.append(gives[4 + part])
     for o in (1, 3, 2):
-        sends[o].wait_recv()
-    plane_10 = joined(y_buf[0], y_buf[1])
-    plane_32 = joined(y_buf[2], y_buf[3])
-    plane = joined(plane_10, plane_32)
+        gives[o].wait_recv()
+    plane_t = [y_buf[k, Q:, :] for k in range(4)]
+    plane_t10 = mm(plane_t[0], plane_t[1])
+    plane_t32 = mm(plane_t[2], plane_t[3])
+    trans = mm(plane_t10, plane_t32)
 
     odd = lax.rem(z, 2) == 1
+    even = jnp.logical_not(odd)
     next_one = {"grp": lax.rem(z + 1, planes)}
     give_state = copy(p_send.at[pl.ds(0, Q)], p_buf.at[pl.ds(0, Q)], p_sem, 0, next_one)
     give_trans = copy(p_send.at[pl.ds(Q, K)], p_buf.at[pl.ds(Q, K)], p_sem, 1, next_one)
     jump = copy(z_out, z_in, z_sem, 0, {"grp": lax.rem(z + 2, planes)})
     step = copy(z_out, z_in, z_sem, 1, next_one)
 
-    @pl.when(jnp.logical_not(odd))
-    def _():
-        p_send[...] = plane
+    @pl.when(even & (z > 0))
+    def _():
+        p_send[Q:, :] = trans
+        give_trans.start()
+
+    for o in (3, 1, 2):
+        gives[4 + o].wait_recv()
+    plane_s = [y_buf[k, :Q, :] for k in range(4)]
+    plane_s10 = mm(plane_s[0], plane_t[1]) + plane_s[1]
+    plane_s32 = mm(plane_s[2], plane_t[3]) + plane_s[3]
+    total = mm(plane_s10, plane_t32) + plane_s32
+
+    @pl.when(even)
+    def _():
+        p_send[:Q, :] = total
         give_state.start()
-        give_trans.start()
-
+
+    row_210[...] = joined(row_10[...], row[2])
+    plane_10 = jnp.concatenate([plane_s10, plane_t10], axis=0)
     plane_210 = joined(plane_10, y_buf[2])
 
     @pl.when(z == 0)
@@ -318,22 +387,22 @@
     @pl.when(z == 1)
     def _():
         give_state.wait_recv()
-        z_out[...] = entered(p_buf[:Q, :], plane)
+        z_out[...] = mm(p_buf[:Q, :], trans) + total
         jump.start()
         step.start()
         enter[...] = p_buf[:Q, :]
+
+    @pl.when(odd & (z > 1))
+    def _():
         give_trans.wait_recv()
-
-    @pl.when(odd & (z > 1))
-    def _():
+        two_t = mm(p_buf[Q:, :], trans)
         give_state.wait_recv()
-        give_trans.wait_recv()
-        two = joined(p_buf[...], plane)
+        two_s = mm(p_buf[:Q, :], trans) + total
         jump.wait_recv()
 
         @pl.when(z < planes - 1)
         def _():
-            z_out[...] = entered(z_in[...], two)
+            z_out[...] = mm(z_in[...], two_t) + two_s
 
             @pl.when(z < planes - 2)
             def _():
@@ -343,7 +412,7 @@
 
         enter[...] = entered(z_in[...], p_buf[...])
 
-    @pl.when(jnp.logical_not(odd) & (z > 0))
+    @pl.when(even & (z > 0))
     def _():
         step.wait_recv()
         enter[...] = z_in[...]
@@ -411,9 +480,12 @@
     for sent in started:
         sent.wait_send()
 
-    @pl.when(jnp.logical_not(odd))
+    @pl.when(even)
     def _():
         give_state.wait_send()
+
+    @pl.when(even & (z > 0))
+    def _():
         give_trans.wait_send()
 
     @pl.when(odd & (z < planes - 1))
@@ -457,8 +529,8 @@
             room(4, ROWS, K),
             room(ROWS, K),
             room(ROWS, K),
-            room(ROWS, K),
-            room(4, Q + K, K),
+            room(K, K),
+            room(4, Q, K),
             room(4, Q + K, K),
             room(Q + K, K),
             room(Q + K, K),
@@ -472,9 +544,9 @@
             room(4, V, K),
             room(H, V, K),
             dma((5,)),
-            dma((2, 4)),
-            dma((2, 4)),
-            dma((2, 4)),
+            dma((2, 8)),
+            dma((2, 15)),
+            dma((2, 8)),
             dma((2, 2)),
             dma((2, 2)),
             dma((2, 4)),

time: 51.6 us -> 46.3 us (0.90)
  Pallas kernels: 50.5 us -> 45.4 us
    pallas_call x1, Pallas kernels: 50.5 us -> 45.4 us  [body(): pl.pallas_call(scan_kernel, out_shape=jax.ShapeDtypeStruct((T, H, V), BF1...]
where the time goes in v2:
time: 46.3 us; the launch traced here: 46.2 us
  Pallas kernels  45.4 us (98%)
  local copies, waits for them, and re-layouts  0.8 us (2%)
    pallas_call x1, Pallas kernels, body(): pl.pallas_call(scan_kernel, out_shape=jax.ShapeDtypeStruct((T, H, V), BF1...  45.4 us

profile of v2, /device:TPU:227, one launch (start us, length us, event | category | flops | bytes accessed | tf_op | source)
XLA Modules:
  0.0 46.2 jit_solution(10481444764073498393)
XLA Ops:
  0.0 45.4 %scan.1 = bf16[128,8,256]{2,1,0:T(8,128)(2,1)S(1)} custom-call(bf16[128,8,128]{2,1,0:T(8,128)(2,1)} %q_ref.1, bf16[128,8,128]{2,1,0:T(8,128)(2,1)} %k_ref.1, bf16[128,8,256]{2,1,0:T(8,128)(2,1)} %v_ref.1, f32[8,128]{1,0:T(8,128)} %lg_ref.1, f32[8,128]{1,0:T(8,128)} %be_ref.1), custom_call_target="tpu_custom_call" | custom-call | tf_op jit(solution)/shard_map/scan/pallas_call | solution.py:507
  45.4 0.8 %copy.7 = bf16[128,8,256]{2,1,0:T(8,128)(2,1)} copy(bf16[128,8,256]{2,1,0:T(8,128)(2,1)S(1)} %scan.1) | data formatting | bytes 1048576

commit v3 on v2

--- a/solution.py
+++ b/solution.py
@@ -19,6 +19,8 @@
 H = 8
 HH = 4
 Q = 64
+NEAR = 16
+PIECES = 2
 ROWS = V + K
 
 
@@ -51,7 +53,11 @@
 
 
 def mm(x, w):
-    return fold(dot(side(x), weights(w)))
+    count = x.shape[0]
+    if count > Q:
+        return fold(dot(side(x), weights(w)))
+    both = fold(dot(jnp.concatenate(split(x), axis=0), side(w)))
+    return both[:count] + both[count:]
 
 
 def mm_nt(x, y):
@@ -108,6 +114,8 @@
     y_buf,
     p_send,
     p_buf,
+    h_send,
+    h_buf,
     z_in,
     z_out,
     enter,
@@ -122,6 +130,7 @@
     xa_sem,
     ya_sem,
     p_sem,
+    h_sem,
     z_sem,
     yb_sem,
     xb_sem,
@@ -145,7 +154,7 @@
     peers = [{"seq_2": 1 - c}]
     peers += [{"seq_1": turn(x, o)} for o in (1, 2, 3)]
     peers += [{"seq_0": turn(y, o)} for o in (1, 2, 3)]
-    peers += [{"grp": lax.rem(z + planes + o, planes)} for o in (1, -1, 2, -2)]
+    peers += [{"grp": lax.rem(z + planes + o, planes)} for o in (1, -1, 2, -2, 3, -3, 4)]
     for peer in peers:
         pl.semaphore_signal(barrier, inc=1, device_id=peer, device_id_type=MESH)
 
@@ -200,13 +209,74 @@
         )
         for h in heads
     ]
-    inverse = [eye - jnp.where(differ == 1, strict[h], 0.0) for h in heads]
-    span = 2
+    near = [jnp.where(differ < NEAR, strict[h], 0.0) for h in heads]
+    inverse = [eye - near[h] for h in heads]
+    power = [mm(near[h], near[h]) for h in heads]
+    reach = 4
+    while reach < NEAR:
+        grown = [
+            mm(jnp.concatenate([inverse[h], power[h]], axis=0), power[h]) for h in heads
+        ]
+        inverse = [inverse[h] + grown[h][:T] for h in heads]
+        power = [grown[h][T:] for h in heads]
+        reach = reach * 2
+    inverse = [inverse[h] + mm(inverse[h], power[h]) for h in heads]
+    span = NEAR
     while span < T:
         level = (differ >= span) & (differ < 2 * span)
-        left = [mm(inverse[h], jnp.where(level, strict[h], 0.0)) for h in heads]
-        inverse = [inverse[h] - mm(left[h], inverse[h]) for h in heads]
+        starts = range(0, T, 2 * span)
+        left = [
+            mm(
+                jnp.concatenate([inverse[h][a : a + span] for a in starts], axis=0),
+                jnp.where(level, strict[h], 0.0),
+            )
+            for h in heads
+        ]
+        change = [mm(left[h], inverse[h]) for h in heads]
+        inverse = [
+            jnp.concatenate(
+                [
+                    piece
+                    for i, a in enumerate(starts)
+                    for piece in (
+                        inverse[h][a : a + span] - change[h][i * span : (i + 1) * span],
+                        inverse[h][a + span : a + 2 * span],
+                    )
+                ],
+                axis=0,
+            )
+            for h in heads
+        ]
         span = span * 2
+    twice = [jnp.concatenate([key_b[h], key_b[h]], axis=0) for h in heads]
+    last = [cum[h : h + 1, T - 1 : T] for h in heads]
+    for h in heads:
+        w_t = fold(dot(key_tb[h], side(inverse[h] * (be_col[h] * rk_col[h]))))
+        moved = dot(side(w_t * (rk_row[h] * -jnp.exp(last[h]))), twice[h])
+        maps[h, V:, :] = moved + eye * jnp.exp(last[h])
+        w_all[h] = w_t
+
+    pl.semaphore_wait(barrier, len(peers))
+
+    order = (2, 1, 3, 0)
+    tail = pl.ds(V, K)
+    body_rows = pl.ds(0, V)
+    swaps = {}
+
+    def swap_cores(i, o, rows):
+        j = turn(x, o)
+        swaps[i + o] = copy(
+            maps.at[HH * (1 - c) + j, rows],
+            pair.at[c, j, rows],
+            core_sem,
+            i + o,
+            {"seq_2": 1 - c},
+        )
+        swaps[i + o].start()
+        started.append(swaps[i + o])
+
+    for o in order:
+        swap_cores(0, o, tail)
     loads[3].wait()
     vf0[...] = v_in[:, :, :K].astype(F32).reshape(T * H, K)
     vf1[...] = v_in[:, :, K:].astype(F32).reshape(T * H, K)
@@ -216,40 +286,12 @@
         value_t = jnp.concatenate(
             [vf0[pl.ds(h, T, stride=H), :].T, vf1[pl.ds(h, T, stride=H), :].T], axis=0
         ).astype(BF16)
-        w_t = fold(dot(key_tb[h], side(inverse[h] * (be_col[h] * rk_col[h]))))
         u_t = fold(dot(value_t, side(inverse[h] * decay_t * be_col[h])))
-        last = cum[h : h + 1, T - 1 : T]
-        into = jnp.concatenate(
-            [
-                u_t * (rk_row[h] * jnp.exp(last - cum_row[h])),
-                w_t * (rk_row[h] * -jnp.exp(last)),
-            ],
-            axis=0,
-        )
-        moved = dot(side(into), jnp.concatenate([key_b[h], key_b[h]], axis=0))
-        maps[h, :V, :] = moved[:V]
-        maps[h, V:, :] = moved[V:] + eye * jnp.exp(last)
-        w_all[h] = w_t
+        scaled = u_t * (rk_row[h] * jnp.exp(last[h] - cum_row[h]))
+        maps[h, :V, :] = dot(side(scaled), twice[h])
         u_all[h] = u_t
-
-    pl.semaphore_wait(barrier, len(peers))
-
-    order = (2, 1, 3, 0)
-    tail = pl.ds(V, K)
-    body_rows = pl.ds(0, V)
-    swaps = {}
-    for i, rows in ((0, tail), (4, body_rows)):
-        for o in order:
-            j = turn(x, o)
-            swaps[i + o] = copy(
-                maps.at[HH * (1 - c) + j, rows],
-                pair.at[c, j, rows],
-                core_sem,
-                i + o,
-                {"seq_2": 1 - c},
-            )
-            swaps[i + o].start()
-            started.append(swaps[i + o])
+    for o in order:
+        swap_cores(4, o, body_rows)
     for o in order:
         j = turn(x, o)
         pair[c, j] = maps[HH * c + j]
@@ -351,13 +393,28 @@
     plane_t32 = mm(plane_t[2], plane_t[3])
     trans = mm(plane_t10, plane_t32)
 
-    odd = lax.rem(z, 2) == 1
-    even = jnp.logical_not(odd)
+    even = lax.rem(z, 2) == 0
     next_one = {"grp": lax.rem(z + 1, planes)}
-    give_state = copy(p_send.at[pl.ds(0, Q)], p_buf.at[pl.ds(0, Q)], p_sem, 0, next_one)
-    give_trans = copy(p_send.at[pl.ds(Q, K)], p_buf.at[pl.ds(Q, K)], p_sem, 1, next_one)
-    jump = copy(z_out, z_in, z_sem, 0, {"grp": lax.rem(z + 2, planes)})
-    step = copy(z_out, z_in, z_sem, 1, next_one)
+    size = Q // PIECES
+    pieces = [pl.ds(i * size, size) for i in range(PIECES)]
+    two_on = {"grp": lax.rem(z + 2, planes)}
+    give_trans = copy(
+        p_send.at[pl.ds(Q, K)], p_buf.at[pl.ds(Q, K)], p_sem, PIECES, next_one
+    )
+    give_state, jump, step = [], [], []
+    for i, rows in enumerate(pieces):
+        give_state.append(copy(p_send.at[rows], p_buf.at[rows], p_sem, i, next_one))
+        jump.append(copy(z_out.at[rows], z_in.at[rows], z_sem, i, two_on))
+        step.append(copy(z_out.at[rows], z_in.at[rows], z_sem, PIECES + i, next_one))
+    far = {}
+    for o in (3, 4):
+        there = {"grp": lax.rem(z + o, planes)}
+        far[o] = [
+            copy(z_out.at[rows], z_in.at[rows], z_sem, (o - 1) * PIECES + i, there)
+            for i, rows in enumerate(pieces)
+        ]
+    hand = {1: copy(h_send, h_buf, h_sem, 0, next_one)}
+    hand[2] = copy(h_send, h_buf, h_sem, 1, two_on)
 
     @pl.when(even & (z > 0))
     def _():
@@ -374,7 +431,8 @@
     @pl.when(even)
     def _():
         p_send[:Q, :] = total
-        give_state.start()
+        for part in give_state:
+            part.start()
 
     row_210[...] = joined(row_10[...], row[2])
     plane_10 = jnp.concatenate([plane_s10, plane_t10], axis=0)
@@ -386,35 +444,64 @@
 
     @pl.when(z == 1)
     def _():
-        give_state.wait_recv()
-        z_out[...] = mm(p_buf[:Q, :], trans) + total
-        jump.start()
-        step.start()
+        for i, rows in enumerate(pieces):
+            give_state[i].wait_recv()
+            z_out[rows, :] = mm(p_buf[rows, :], trans) + total[i * size : (i + 1) * size]
+            jump[i].start()
+        for part in step:
+            part.start()
         enter[...] = p_buf[:Q, :]
 
-    @pl.when(odd & (z > 1))
+    @pl.when(z == 3)
     def _():
         give_trans.wait_recv()
         two_t = mm(p_buf[Q:, :], trans)
-        give_state.wait_recv()
+        for part in give_state:
+            part.wait_recv()
         two_s = mm(p_buf[:Q, :], trans) + total
-        jump.wait_recv()
-
-        @pl.when(z < planes - 1)
-        def _():
-            z_out[...] = mm(z_in[...], two_t) + two_s
-
-            @pl.when(z < planes - 2)
-            def _():
-                jump.start()
-
-            step.start()
-
+        for i, rows in enumerate(pieces):
+            jump[i].wait_recv()
+            z_out[rows, :] = mm(z_in[rows, :], two_t) + two_s[i * size : (i + 1) * size]
+            far[4][i].start()
+        for part in far[3] + jump + step:
+            part.start()
         enter[...] = entered(z_in[...], p_buf[...])
 
-    @pl.when(even & (z > 0))
-    def _():
-        step.wait_recv()
+    @pl.when(z == 5)
+    def _():
+        give_trans.wait_recv()
+        h_send[Q:, :] = mm(p_buf[Q:, :], trans)
+        for part in give_state:
+            part.wait_recv()
+        h_send[:Q, :] = mm(p_buf[:Q, :], trans) + total
+        hand[2].start()
+        hand[1].start()
+        for part in jump:
+            part.wait_recv()
+        enter[...] = entered(z_in[...], p_buf[...])
+
+    @pl.when(z == 6)
+    def _():
+        hand[1].wait_recv()
+        for part in far[3]:
+            part.wait_recv()
+        enter[...] = entered(z_in[...], h_buf[...])
+
+    @pl.when(z == 7)
+    def _():
+        give_trans.wait_recv()
+        for part in give_state:
+            part.wait_recv()
+        hand[2].wait_recv()
+        three = joined(h_buf[...], p_buf[...])
+        for part in far[4]:
+            part.wait_recv()
+        enter[...] = entered(z_in[...], three)
+
+    @pl.when((z == 2) | (z == 4))
+    def _():
+        for part in step:
+            part.wait_recv()
         enter[...] = z_in[...]
 
     state = enter[...]
@@ -482,19 +569,27 @@
 
     @pl.when(even)
     def _():
-        give_state.wait_send()
+        for part in give_state:
+            part.wait_send()
 
     @pl.when(even & (z > 0))
     def _():
         give_trans.wait_send()
 
-    @pl.when(odd & (z < planes - 1))
-    def _():
-        step.wait_send()
-
-    @pl.when(odd & (z < planes - 2))
-    def _():
-        jump.wait_send()
+    @pl.when((z == 1) | (z == 3))
+    def _():
+        for part in jump + step:
+            part.wait_send()
+
+    @pl.when(z == 3)
+    def _():
+        for part in far[3] + far[4]:
+            part.wait_send()
+
+    @pl.when(z == 5)
+    def _():
+        hand[1].wait_send()
+        hand[2].wait_send()
 
 
 def body(*given):
@@ -534,6 +629,8 @@
             room(4, Q + K, K),
             room(Q + K, K),
             room(Q + K, K),
+            room(Q + K, K),
+            room(Q + K, K),
             room(Q, K),
             room(Q, K),
             room(Q, K),
@@ -547,8 +644,9 @@
             dma((2, 8)),
             dma((2, 15)),
             dma((2, 8)),
+            dma((2, PIECES + 1)),
             dma((2, 2)),
-            dma((2, 2)),
+            dma((2, 4 * PIECES)),
             dma((2, 4)),
             dma((2, 16)),
             dma((2, 4)),

time: 46.3 us -> 44.8 us (0.968)
  Pallas kernels: 45.4 us -> 43.8 us
    pallas_call x1, Pallas kernels: 45.4 us -> 43.8 us  [body(): pl.pallas_call(scan_kernel, out_shape=jax.ShapeDtypeStruct((T, H, V), BF1...]
where the time goes in v3:
time: 44.8 us; the launch traced here: 44.6 us
  Pallas kernels  43.8 us (98%)
  local copies, waits for them, and re-layouts  0.8 us (2%)
    pallas_call x1, Pallas kernels, body(): pl.pallas_call(scan_kernel, out_shape=jax.ShapeDtypeStruct((T, H, V), BF1...  43.8 us

profile of v3, /device:TPU:227, one launch (start us, length us, event | category | flops | bytes accessed | tf_op | source)
XLA Modules:
  0.0 44.6 jit_solution(15661518508239655544)
XLA Ops:
  0.0 43.8 %scan.1 = bf16[128,8,256]{2,1,0:T(8,128)(2,1)S(1)} custom-call(bf16[128,8,128]{2,1,0:T(8,128)(2,1)} %q_ref.1, bf16[128,8,128]{2,1,0:T(8,128)(2,1)} %k_ref.1, bf16[128,8,256]{2,1,0:T(8,128)(2,1)} %v_ref.1, f32[8,128]{1,0:T(8,128)} %lg_ref.1, f32[8,128]{1,0:T(8,128)} %be_ref.1), custom_call_target="tpu_custom_call" | custom-call | tf_op jit(solution)/shard_map/scan/pallas_call | solution.py:602
  43.8 0.8 %copy.7 = bf16[128,8,256]{2,1,0:T(8,128)(2,1)} copy(bf16[128,8,256]{2,1,0:T(8,128)(2,1)S(1)} %scan.1) | data formatting | bytes 1048576

commit v4 on v3

--- a/solution.py
+++ b/solution.py
@@ -20,6 +20,20 @@
 HH = 4
 Q = 64
 NEAR = 16
+LINKED = (
+    (0, 1),
+    (1, 2),
+    (1, 3),
+    (2, 3),
+    (3, 4),
+    (3, 5),
+    (3, 6),
+    (3, 7),
+    (4, 5),
+    (5, 6),
+    (5, 7),
+    (6, 7),
+)
 PIECES = 2
 ROWS = V + K
 
@@ -154,9 +168,18 @@
     peers = [{"seq_2": 1 - c}]
     peers += [{"seq_1": turn(x, o)} for o in (1, 2, 3)]
     peers += [{"seq_0": turn(y, o)} for o in (1, 2, 3)]
-    peers += [{"grp": lax.rem(z + planes + o, planes)} for o in (1, -1, 2, -2, 3, -3, 4)]
     for peer in peers:
         pl.semaphore_signal(barrier, inc=1, device_id=peer, device_id_type=MESH)
+    greeted = jnp.int32(len(peers))
+    for low, high in LINKED:
+        for at, o in ((low, high - low), (high, low - high)):
+            greeted = greeted + jnp.where(z == at, 1, 0)
+
+            @pl.when(z == at)
+            def _():
+                there = {"grp": lax.rem(z + planes + o, planes)}
+                pl.semaphore_signal(barrier, inc=1, device_id=there, device_id_type=MESH)
+
 
     def copy(src, dst, sem, o, peer):
         return pltpu.make_async_remote_copy(
@@ -256,7 +279,7 @@
         maps[h, V:, :] = moved + eye * jnp.exp(last[h])
         w_all[h] = w_t
 
-    pl.semaphore_wait(barrier, len(peers))
+    pl.semaphore_wait(barrier, greeted)
 
     order = (2, 1, 3, 0)
     tail = pl.ds(V, K)

time: 44.8 us -> 43.6 us (0.973); the launches traced: 44.6 us -> 42.8 us
  Pallas kernels: 43.8 us -> 42 us
    pallas_call x1, Pallas kernels: 43.8 us -> 42 us  [body(): pl.pallas_call(scan_kernel, out_shape=jax.ShapeDtypeStruct((T, H, V), BF1...]
where the time goes in v4:
time: 43.6 us; the launch traced here: 42.8 us
  Pallas kernels  42 us (96%)
  local copies, waits for them, and re-layouts  0.8 us (2%)
    pallas_call x1, Pallas kernels, body(): pl.pallas_call(scan_kernel, out_shape=jax.ShapeDtypeStruct((T, H, V), BF1...  42 us

profile of v4, /device:TPU:227, one launch (start us, length us, event | category | flops | bytes accessed | tf_op | source)
XLA Modules:
  0.0 42.8 jit_solution(7663934396228934010)
XLA Ops:
  0.0 42.0 %scan.1 = bf16[128,8,256]{2,1,0:T(8,128)(2,1)S(1)} custom-call(bf16[128,8,128]{2,1,0:T(8,128)(2,1)} %q_ref.1, bf16[128,8,128]{2,1,0:T(8,128)(2,1)} %k_ref.1, bf16[128,8,256]{2,1,0:T(8,128)(2,1)} %v_ref.1, f32[8,128]{1,0:T(8,128)} %lg_ref.1, f32[8,128]{1,0:T(8,128)} %be_ref.1), custom_call_target="tpu_custom_call" | custom-call | tf_op jit(solution)/shard_map/scan/pallas_call | solution.py:625
  42.0 0.8 %copy.7 = bf16[128,8,256]{2,1,0:T(8,128)(2,1)} copy(bf16[128,8,256]{2,1,0:T(8,128)(2,1)S(1)} %scan.1) | data formatting | bytes 1048576

commit v5 on v4

--- a/solution.py
+++ b/solution.py
@@ -71,6 +71,12 @@
     if count > Q:
         return fold(dot(side(x), weights(w)))
     both = fold(dot(jnp.concatenate(split(x), axis=0), side(w)))
+    return both[:count] + both[count:]
+
+
+def through(x, sided):
+    count = x.shape[0]
+    both = fold(dot(jnp.concatenate(split(x), axis=0), sided))
     return both[:count] + both[count:]
 
 
@@ -460,6 +466,8 @@
     row_210[...] = joined(row_10[...], row[2])
     plane_10 = jnp.concatenate([plane_s10, plane_t10], axis=0)
     plane_210 = joined(plane_10, y_buf[2])
+    down_y = [side(plane_t[0]), side(plane_t10), side(plane_210[Q:])]
+    down_x = [side(row_t[0]), side(row_t10), side(row_210[V:, :])]
 
     @pl.when(z == 0)
     def _():
@@ -529,9 +537,9 @@
 
     state = enter[...]
     r_send[0] = state
-    r_send[1] = entered(state, y_buf[0])
-    r_send[2] = entered(state, plane_10)
-    r_send[3] = entered(state, plane_210)
+    r_send[1] = through(state, down_y[0]) + plane_s[0]
+    r_send[2] = through(state, down_y[1]) + plane_s10
+    r_send[3] = through(state, down_y[2]) + plane_210[:Q]
     mine = pl.ds(pl.multiple_of(y * Q, Q), Q)
     sends = {}
     for o in (2, 1, 3):
@@ -547,9 +555,9 @@
         part = pl.ds(pl.multiple_of(turn(y, -o) * Q, Q), Q)
         state = r_buf[part, :]
         x_send[0, part, :] = state
-        x_send[1, part, :] = mm(state, row[0, V:, :]) + row[0, part, :]
-        x_send[2, part, :] = mm(state, row_10[V:, :]) + row_10[part, :]
-        x_send[3, part, :] = mm(state, row_210[V:, :]) + row_210[part, :]
+        x_send[1, part, :] = through(state, down_x[0]) + row[0, part, :]
+        x_send[2, part, :] = through(state, down_x[1]) + row_10[part, :]
+        x_send[3, part, :] = through(state, down_x[2]) + row_210[part, :]
         for a in (2, 1, 3):
             to = turn(x, a)
             sent = copy(

time: 43.6 us -> 43.6 us (level)
  no operation moved by 1% of the time
where the time goes in v5:
time: 43.6 us; the launch traced here: 42.8 us
  Pallas kernels  42 us (96%)
  local copies, waits for them, and re-layouts  0.8 us (2%)
    pallas_call x1, Pallas kernels, body(): pl.pallas_call(scan_kernel, out_shape=jax.ShapeDtypeStruct((T, H, V), BF1...  42 us

profile of v5, /device:TPU:227, one launch (start us, length us, event | category | flops | bytes accessed | tf_op | source)
XLA Modules:
  0.0 42.8 jit_solution(14832273439088287175)
XLA Ops:
  0.0 42.0 %scan.1 = bf16[128,8,256]{2,1,0:T(8,128)(2,1)S(1)} custom-call(bf16[128,8,128]{2,1,0:T(8,128)(2,1)} %q_ref.1, bf16[128,8,128]{2,1,0:T(8,128)(2,1)} %k_ref.1, bf16[128,8,256]{2,1,0:T(8,128)(2,1)} %v_ref.1, f32[8,128]{1,0:T(8,128)} %lg_ref.1, f32[8,128]{1,0:T(8,128)} %be_ref.1), custom_call_target="tpu_custom_call" | custom-call | tf_op jit(solution)/shard_map/scan/pallas_call | solution.py:633
  42.0 0.8 %copy.7 = bf16[128,8,256]{2,1,0:T(8,128)(2,1)} copy(bf16[128,8,256]{2,1,0:T(8,128)(2,1)S(1)} %scan.1) | data formatting | bytes 1048576
